TPU v7x, 32 devices: a whole 2x2x4 slice. The times are simulated.
32 devices in a mesh: seg: 16 (over z, x, core), freq: 2 (over y).
Axes of the slice: x: 2, y: 2, z: 4, core: 2. Of those that a mesh axis runs over, the one named last changes fastest.
Arguments:
- coarse: float32 [64, 128, 2048], P('seg', None, 'freq'), may hold values from 0.5 to 8
- offsets: int32 [64, 32], replicated, may hold values from -8 to 8, as said below
Outputs:
- fine: float32 [32, 128, 2048], P(None, 'seg', 'freq')
- peaks: float32 [128], P('seg')
Inputs may be any that keep to these rules, and one draw needn't show every extreme that they name: `offsets`: every entry lies in -8 to 8, and both ends occur in every draw.
All inputs are finite; a program needn't handle non-finite values.
Results may differ from a plain program's by a relative error of at most 0.0003.
Values sent between devices are 32-bit elements; how exact they have to be, the bound alone decides.
A program may use at most 128 MiB of HBM per device.

v0:
```python
import jax
import jax.numpy as jnp
from jax import lax
from jax.sharding import PartitionSpec as P

HALO = 8


def extended(block, sides, width):
    for axis, dim in sides:
        count = lax.axis_size(axis)
        forward = [(i, i + 1) for i in range(count - 1)]
        backward = [(target, source) for source, target in forward]
        low = lax.ppermute(
            lax.slice_in_dim(block, block.shape[dim] - width, None, axis=dim), axis, forward
        )
        high = lax.ppermute(lax.slice_in_dim(block, 0, width, axis=dim), axis, backward)
        block = jnp.concatenate([low, block, high], axis=dim)
    return block


def shift_sum(padded, offsets):
    seg_count, point_count, wide_bins = padded.shape
    bin_count = wide_bins - 2 * HALO
    spin_count = offsets.shape[1]
    columns = offsets.T
    total = jnp.zeros((spin_count, point_count, bin_count), jnp.float32)
    for shift in range(-HALO, HALO + 1):
        weights = (columns == shift).astype(jnp.float32) / seg_count
        product = jnp.einsum(
            "ks,spw->kpw",
            weights,
            padded,
            precision=lax.Precision.HIGHEST,
            preferred_element_type=jnp.float32,
        )
        total = total + product[:, :, HALO + shift : HALO + shift + bin_count]
    return total


def on_device(coarse, offsets):
    nseg = lax.axis_size("seg")
    local_segs, points, bins_local = coarse.shape
    blocks = coarse.reshape(local_segs, nseg, points // nseg, bins_local)
    maps = lax.all_to_all(blocks, "seg", split_axis=1, concat_axis=0, tiled=True)[:, 0]
    padded = extended(maps, (("freq", 2),), HALO)
    fine_part = shift_sum(padded, offsets)
    top = jnp.max(fine_part, axis=(0, 2))
    top_rows = top[None, :]
    peaks = lax.pmax(top_rows[0], "freq")
    return (fine_part, peaks)


def solution(mesh):
    return jax.shard_map(
        on_device,
        mesh=mesh,
        in_specs=(P("seg", None, "freq"), P()),
        out_specs=(P(None, "seg", "freq"), P("seg")),
        check_vma=False,
    )
```

profile of v0, /device:TPU:8, one launch (start us, length us, event | category | flops | bytes accessed | tf_op | source)
XLA Modules:
  0.0 123.9 jit_solution(5264826384109288362)
XLA Ops:
  0.6 2.9 %copy.6 = f32[4,128,1024]{2,0,1:T(4,128)S(1)} copy(f32[4,128,1024]{2,1,0:T(8,128)} %param.2) | data formatting | bytes 4194304 | tf_op args[0]
  3.6 53.3 %all_to_all.15 = f32[4,16,8,1024]{3,0,2,1:T(4,128)S(1)} all-to-all(f32[4,16,8,1024]{3,0,2,1:T(4,128)S(1)} %bitcast.61), channel_id=1, replica_groups=mesh['seg'=16,'freq'=2] {'seg'}, dimensions={1} | all-to-all | bytes 4194304 | tf_op jit(solution)/shard_map/all_to_all | solution.py:45
  58.3 2.0 %squeeze.3 = f32[64,8,1024]{2,0,1:T(8,128)S(1)} reshape(f32[16,4,1,8,1024]{4,1,0,3,2:T(4,128)} %copy.7) | data formatting | bytes 4194304 | tf_op jit(solution)/shard_map/squeeze | solution.py:45
  61.2 4.1 %collective-permute-start = (f32[64,8,8]{2,0,1:T(8,128)S(1)}, f32[64,8,8]{2,0,1:T(8,128)}, u32[]{:S(2)}, u32[]{:S(2)}) collective-permute-start(f32[64,8,8]{2,0,1:T(8,128)S(1)} %get-tuple-element.6), channel_id=1, source_target_pairs={{0,1},{2,3},{4,5},{6,7},{8,9},{10,11},{12,13},{14,15},{16,17},{18,... | collective-permute-start | bytes 49160 | tf_op jit(solution)/shard_map/ppermute | solution.py:14
  68.0 3.1 %collective-permute-done = f32[64,8,8]{2,0,1:T(8,128)} collective-permute-done((f32[64,8,8]{2,0,1:T(8,128)S(1)}, f32[64,8,8]{2,0,1:T(8,128)}, u32[]{:S(2)}, u32[]{:S(2)}) %collective-permute-start) | collective-permute-done | bytes 16416 | tf_op jit(solution)/shard_map/ppermute | solution.py:14
  71.1 3.0 %concatenate.4 = f32[64,8,1032]{2,0,1:T(8,128)S(1)} concatenate(f32[64,8,8]{2,0,1:T(8,128)} %collective-permute-done, f32[64,8,1024]{2,0,1:T(8,128)} %copy-done.1), dimensions={2} | concatenate | bytes 4227072 | tf_op jit(solution)/shard_map/concatenate | solution.py:18
  74.1 2.5 %fusion.16 = f32[32,8,1024]{2,0,1:T(8,128)} fusion(f32[64,8,1032]{2,0,1:T(8,128)S(1)} %concatenate.4, s32[64,32]{0,1:T(8,128)S(1)} %copy-done.2), kind=kOutput, calls=%fused_computation.16 | convolution fusion | flops 201330688 | bytes 3162112 | tf_op jit(solution)/shard_map/ks,spw->kpw/dot_general | solution.py:30
  76.7 2.6 %fusion.18 = f32[32,8,1024]{2,0,1:T(8,128)} fusion(f32[64,8,1032]{2,0,1:T(8,128)S(1)} %concatenate.4, s32[64,32]{0,1:T(8,128)S(1)} %copy-done.2), kind=kOutput, calls=%fused_computation.18 | convolution fusion | flops 201330688 | bytes 3162112 | tf_op jit(solution)/shard_map/ks,spw->kpw/dot_general | solution.py:30
  79.2 2.6 %fusion.20 = f32[32,8,1024]{2,0,1:T(8,128)} fusion(f32[64,8,1032]{2,0,1:T(8,128)S(1)} %concatenate.4, s32[64,32]{0,1:T(8,128)S(1)} %copy-done.2), kind=kOutput, calls=%fused_computation.20 | convolution fusion | flops 201330688 | bytes 3162112 | tf_op jit(solution)/shard_map/ks,spw->kpw/dot_general | solution.py:30
  81.8 2.5 %fusion.22 = f32[32,8,1024]{2,0,1:T(8,128)} fusion(f32[64,8,1032]{2,0,1:T(8,128)S(1)} %concatenate.4, s32[64,32]{0,1:T(8,128)S(1)} %copy-done.2), kind=kOutput, calls=%fused_computation.22 | convolution fusion | flops 201330688 | bytes 3162112 | tf_op jit(solution)/shard_map/ks,spw->kpw/dot_general | solution.py:30
  84.3 2.6 %fusion.24 = f32[32,8,1024]{2,0,1:T(8,128)} fusion(f32[64,8,1032]{2,0,1:T(8,128)S(1)} %concatenate.4, s32[64,32]{0,1:T(8,128)S(1)} %copy-done.2), kind=kOutput, calls=%fused_computation.24 | convolution fusion | flops 201330688 | bytes 3162112 | tf_op jit(solution)/shard_map/ks,spw->kpw/dot_general | solution.py:30
  87.0 2.6 %fusion.26 = f32[32,8,1024]{2,0,1:T(8,128)} fusion(f32[64,8,1032]{2,0,1:T(8,128)S(1)} %concatenate.4, s32[64,32]{0,1:T(8,128)S(1)} %copy-done.2), kind=kOutput, calls=%fused_computation.26 | convolution fusion | flops 201330688 | bytes 3162112 | tf_op jit(solution)/shard_map/ks,spw->kpw/dot_general | solution.py:30
  89.6 2.6 %fusion.28 = f32[32,8,1024]{2,0,1:T(8,128)} fusion(f32[64,8,1032]{2,0,1:T(8,128)S(1)} %concatenate.4, s32[64,32]{0,1:T(8,128)S(1)} %copy-done.2), kind=kOutput, calls=%fused_computation.28 | convolution fusion | flops 201330688 | bytes 3162112 | tf_op jit(solution)/shard_map/ks,spw->kpw/dot_general | solution.py:30
  92.2 7.3 %concatenate.12 = f32[64,8,1032]{2,0,1:T(8,128)} concatenate(f32[64,8,1024]{2,0,1:T(8,128)} %copy-done.1, f32[64,8,8]{2,0,1:T(8,128)} %collective-permute-done.1), dimensions={2} | concatenate | bytes 4227072 | tf_op jit(solution)/shard_map/concatenate | solution.py:18
  99.5 3.4 %fusion = f32[32,8,1024]{2,0,1:T(8,128)S(1)} fusion(f32[64,8,1032]{2,0,1:T(8,128)} %concatenate.12, s32[64,32]{0,1:T(8,128)S(1)} %copy-done.2), kind=kOutput, calls=%fused_computation | convolution fusion | flops 201330688 | bytes 3153920 | tf_op jit(solution)/shard_map/ks,spw->kpw/dot_general | solution.py:30
  102.9 1.6 %fusion.2 = f32[32,8,1024]{2,0,1:T(8,128)S(1)} fusion(f32[64,8,1032]{2,0,1:T(8,128)S(1)} %copy-done, s32[64,32]{0,1:T(8,128)S(1)} %copy-done.2), kind=kOutput, calls=%fused_computation.2 | convolution fusion | flops 201330688 | bytes 3162112 | tf_op jit(solution)/shard_map/ks,spw->kpw/dot_general | solution.py:30
  104.5 1.6 %fusion.4 = f32[32,8,1024]{2,0,1:T(8,128)S(1)} fusion(f32[64,8,1032]{2,0,1:T(8,128)S(1)} %copy-done, s32[64,32]{0,1:T(8,128)S(1)} %copy-done.2), kind=kOutput, calls=%fused_computation.4 | convolution fusion | flops 201330688 | bytes 3162112 | tf_op jit(solution)/shard_map/ks,spw->kpw/dot_general | solution.py:30
  106.0 1.6 %fusion.6 = f32[32,8,1024]{2,0,1:T(8,128)S(1)} fusion(f32[64,8,1032]{2,0,1:T(8,128)S(1)} %copy-done, s32[64,32]{0,1:T(8,128)S(1)} %copy-done.2), kind=kOutput, calls=%fused_computation.6 | convolution fusion | flops 201330688 | bytes 3162112 | tf_op jit(solution)/shard_map/ks,spw->kpw/dot_general | solution.py:30
  107.6 1.6 %fusion.8 = f32[32,8,1024]{2,0,1:T(8,128)S(1)} fusion(f32[64,8,1032]{2,0,1:T(8,128)S(1)} %copy-done, s32[64,32]{0,1:T(8,128)S(1)} %copy-done.2), kind=kOutput, calls=%fused_computation.8 | convolution fusion | flops 201330688 | bytes 3162112 | tf_op jit(solution)/shard_map/ks,spw->kpw/dot_general | solution.py:30
  109.2 1.6 %fusion.10 = f32[32,8,1024]{2,0,1:T(8,128)S(1)} fusion(f32[64,8,1032]{2,0,1:T(8,128)S(1)} %copy-done, s32[64,32]{0,1:T(8,128)S(1)} %copy-done.2), kind=kOutput, calls=%fused_computation.10 | convolution fusion | flops 201330688 | bytes 3162112 | tf_op jit(solution)/shard_map/ks,spw->kpw/dot_general | solution.py:30
  110.8 1.6 %fusion.12 = f32[32,8,1024]{2,0,1:T(8,128)S(1)} fusion(f32[64,8,1032]{2,0,1:T(8,128)S(1)} %copy-done, s32[64,32]{0,1:T(8,128)S(1)} %copy-done.2), kind=kOutput, calls=%fused_computation.12 | convolution fusion | flops 201330688 | bytes 3162112 | tf_op jit(solution)/shard_map/ks,spw->kpw/dot_general | solution.py:30
  114.3 2.0 %fusion.235 = (f32[8]{0:T(128)S(1)}, f32[32,8,1024]{2,0,1:T(8,128)S(1)}) fusion(f32[32,8,1024]{2,0,1:T(8,128)S(1)} %fusion, f32[32,8,1024]{2,0,1:T(8,128)S(1)} %fusion.2, f32[32,8,1024]{2,0,1:T(8,128)S(1)} %fusion.4, f32[32,8,1024]{2,0,1:T(8,128)S(1)} %fusion.6, f32[32,8,1024]{2,0,1:T(8,128)S(1)} %fusion.8, f32[32,8,1024]{2,0,1:T(8,128)S(1)} %fusion.10, ...), kind=kOutput, calls=%fused_computation.203 | convolution fusion | flops 203689984 | bytes 11550752 | tf_op jit(solution)/shard_map/ks,spw->kpw/dot_general | solution.py:30
  116.3 6.0 %pmax.7 = f32[8]{0:T(128)} all-reduce(f32[8]{0:T(128)S(1)} %get-tuple-element.8), channel_id=1, replica_groups=mesh['seg'=16,'freq'=2] {'freq'}, use_global_device_ids=true, to_apply=%region_1.0 | all-reduce | flops 8 | bytes 64 | tf_op jit(solution)/shard_map/pmax | solution.py:50
  122.3 1.6 %copy.8 = f32[32,8,1024]{2,1,0:T(8,128)} copy(f32[32,8,1024]{2,0,1:T(8,128)S(1)} %get-tuple-element.9) | data formatting | bytes 2097152
  (26 shorter events, 6.8 us)
Async XLA Ops:
  58.3 8.5 %copy-start.2 = (s32[64,32]{0,1:T(8,128)S(1)}, s32[64,32]{0,1:T(8,128)}, u32[]{:S(2)}) copy-start(s32[64,32]{0,1:T(8,128)} %param.3) | copy-start | bytes 24580
  60.3 7.6 %copy-start.1 = (f32[64,8,1024]{2,0,1:T(8,128)}, f32[64,8,1024]{2,0,1:T(8,128)S(1)}, u32[]{:S(2)}) copy-start(f32[64,8,1024]{2,0,1:T(8,128)S(1)} %squeeze.3) | copy-start | bytes 6291460
  61.2 9.9 %collective-permute-start = (f32[64,8,8]{2,0,1:T(8,128)S(1)}, f32[64,8,8]{2,0,1:T(8,128)}, u32[]{:S(2)}, u32[]{:S(2)}) collective-permute-start(f32[64,8,8]{2,0,1:T(8,128)S(1)} %get-tuple-element.6), channel_id=1, source_target_pairs={{0,1},{2,3},{4,5},{6,7},{8,9},{10,11},{12,13},{14,15},{16,17},{18,... | collective-permute-start | bytes 49160 | tf_op jit(solution)/shard_map/ppermute | solution.py:14
  65.4 26.8 %collective-permute-start.1 = (f32[64,8,8]{2,0,1:T(8,128)}, f32[64,8,8]{2,0,1:T(8,128)}, u32[]{:S(2)}, u32[]{:S(2)}) collective-permute-start(f32[64,8,8]{2,0,1:T(8,128)} %get-tuple-element.7), channel_id=1, source_target_pairs={{1,0},{3,2},{5,4},{7,6},{9,8},{11,10},{13,12},{15,14},{17,16},{19,... | collective-permute-start | bytes 49160 | tf_op jit(solution)/shard_map/ppermute | solution.py:17
  99.5 3.4 %copy-start = (f32[64,8,1032]{2,0,1:T(8,128)S(1)}, f32[64,8,1032]{2,0,1:T(8,128)}, u32[]{:S(2)}) copy-start(f32[64,8,1032]{2,0,1:T(8,128)} %concatenate.12) | copy-start | bytes 6340612
  107.6 4.8 %copy-start.9 = (f32[32,8,1024]{2,0,1:T(8,128)S(1)}, f32[32,8,1024]{2,0,1:T(8,128)}, u32[]{:S(2)}) copy-start(f32[32,8,1024]{2,0,1:T(8,128)} %fusion.28) | copy-start | bytes 3145732
  109.2 3.2 %copy-start.6 = (f32[32,8,1024]{2,0,1:T(8,128)S(1)}, f32[32,8,1024]{2,0,1:T(8,128)}, u32[]{:S(2)}) copy-start(f32[32,8,1024]{2,0,1:T(8,128)} %fusion.22) | copy-start | bytes 3145732
  109.2 3.2 %copy-start.7 = (f32[32,8,1024]{2,0,1:T(8,128)S(1)}, f32[32,8,1024]{2,0,1:T(8,128)}, u32[]{:S(2)}) copy-start(f32[32,8,1024]{2,0,1:T(8,128)} %fusion.24) | copy-start | bytes 3145732
  109.2 3.2 %copy-start.8 = (f32[32,8,1024]{2,0,1:T(8,128)S(1)}, f32[32,8,1024]{2,0,1:T(8,128)}, u32[]{:S(2)}) copy-start(f32[32,8,1024]{2,0,1:T(8,128)} %fusion.26) | copy-start | bytes 3145732
  110.8 1.7 %copy-start.3 = (f32[32,8,1024]{2,0,1:T(8,128)S(1)}, f32[32,8,1024]{2,0,1:T(8,128)}, u32[]{:S(2)}) copy-start(f32[32,8,1024]{2,0,1:T(8,128)} %fusion.16) | copy-start | bytes 3145732
  110.8 1.7 %copy-start.4 = (f32[32,8,1024]{2,0,1:T(8,128)S(1)}, f32[32,8,1024]{2,0,1:T(8,128)}, u32[]{:S(2)}) copy-start(f32[32,8,1024]{2,0,1:T(8,128)} %fusion.18) | copy-start | bytes 3145732
  110.8 1.9 %copy-start.5 = (f32[32,8,1024]{2,0,1:T(8,128)S(1)}, f32[32,8,1024]{2,0,1:T(8,128)}, u32[]{:S(2)}) copy-start(f32[32,8,1024]{2,0,1:T(8,128)} %fusion.20) | copy-start | bytes 3145732
where the time goes:
time: 126 us; the launch traced here: 124 us
  blocking collectives  59.2 us (47%)
  matrix products  35.6 us (28%)
  local copies, waits for them, and re-layouts  19.5 us (15%)
  starting transfers between devices  5.59 us (4%)
  waiting for transfers between devices  3.14 us (2%)
    all_to_all x1, blocking collectives, on_device(): lax.all_to_all(blocks, 'seg', split_axis=1, concat_axis=0, tiled=True)[:, 0]  53.3 us
    dot_general x17, matrix products, shift_sum(): jnp.einsum('ks,spw->kpw', weights, padded, precision=lax.Precision.HIGHES...  35.6 us
    concatenate x2, local copies, waits for them, and re-layouts, extended(): block = jnp.concatenate([low, block, high], axis=dim)  10.3 us
    pmax x1, blocking collectives, on_device(): peaks = lax.pmax(top_rows[0], 'freq')  5.97 us
    unnamed x22, local copies, waits for them, and re-layouts  4.8 us
    ppermute x1, starting transfers between devices, extended(): lax.ppermute(lax.slice_in_dim(block, block.shape[dim] - width, None, axis...  4.13 us
    ppermute x1, waiting for transfers between devices, extended(): lax.ppermute(lax.slice_in_dim(block, block.shape[dim] - width, None, axis...  3.14 us
  transfers between devices with their start and end apart: 2, of which 1 were waited for; matrix products, arithmetic and copies ran while one was open for 18% of the time, Pallas kernels for 0%

commit v1 on v0

v1 whole, which is shorter than its diff:
```python
import functools

import jax
import jax.numpy as jnp
from jax import lax
from jax.experimental import pallas as pl
from jax.experimental.pallas import tpu as pltpu
from jax.sharding import PartitionSpec as P

HALO = 8
EDGE = 128
SHIFTS = 2 * HALO + 1
MESH = pl.DeviceIdType.MESH


def partner(me, step, count):
    if count & (count - 1):
        return lax.rem(step + count - me, count)
    result = me
    bit = 1
    while bit < count:
        wanted = lax.rem(step // bit, 2)
        held = lax.rem(me // bit, 2)
        result = result + bit * wanted * (1 - 2 * held)
        bit *= 2
    return result


def kernel(
    nseg,
    nfreq,
    coarse,
    offsets,
    total,
    peaks,
    maps,
    low,
    high,
    shifted,
    tops,
    own_sem,
    send_sem,
    recv_sem,
    up_send,
    up_recv,
    down_send,
    down_recv,
    top_send,
    top_recv,
):
    local_segs = coarse.shape[0]
    spins, rows, bins = total.shape
    me = lax.axis_index("seg")
    band = lax.axis_index("freq")

    def mine(target):
        return coarse.at[:, pl.ds(pl.multiple_of(target * rows, rows), rows), :]

    def exchange(step):
        other = partner(me, step, nseg)
        return pltpu.make_async_remote_copy(
            src_ref=mine(other),
            dst_ref=maps.at[step],
            send_sem=send_sem.at[step],
            recv_sem=recv_sem.at[step],
            device_id={"seg": other, "freq": band},
            device_id_type=MESH,
        )

    def upward(step):
        return pltpu.make_async_remote_copy(
            src_ref=maps.at[step, :, :, pl.ds(bins - EDGE, EDGE)],
            dst_ref=low.at[step],
            send_sem=up_send.at[step],
            recv_sem=up_recv.at[step],
            device_id={"seg": me, "freq": band + 1},
            device_id_type=MESH,
        )

    def downward(step):
        return pltpu.make_async_remote_copy(
            src_ref=maps.at[step, :, :, pl.ds(0, EDGE)],
            dst_ref=high.at[step],
            send_sem=down_send.at[step],
            recv_sem=down_recv.at[step],
            device_id={"seg": me, "freq": band - 1},
            device_id_type=MESH,
        )

    own = pltpu.make_async_copy(mine(me), maps.at[0], own_sem)
    own.start()

    barrier = pltpu.get_barrier_semaphore()

    @pl.loop(1, nseg)
    def _(step):
        pl.semaphore_signal(
            barrier, inc=1, device_id={"seg": partner(me, step, nseg), "freq": band}, device_id_type=MESH
        )

    for step in range(1, nfreq):
        pl.semaphore_signal(
            barrier, inc=1, device_id={"seg": me, "freq": lax.rem(band + step, nfreq)}, device_id_type=MESH
        )

    total[...] = jnp.zeros_like(total)

    @pl.when(band == 0)
    def _():
        low[...] = jnp.zeros_like(low)

    @pl.when(band == nfreq - 1)
    def _():
        high[...] = jnp.zeros_like(high)

    pl.semaphore_wait(barrier, nseg - 1 + nfreq - 1)

    @pl.loop(1, nseg)
    def _(step):
        exchange(step).start()

    def forward(step):
        @pl.when(band < nfreq - 1)
        def _():
            upward(step).start()

        @pl.when(band > 0)
        def _():
            downward(step).start()

    def add(step):
        @pl.when(band < nfreq - 1)
        def _():
            downward(step).wait_recv()

        @pl.when(band > 0)
        def _():
            upward(step).wait_recv()

        first = partner(me, step, nseg) * local_segs
        lane = lax.broadcasted_iota(jnp.int32, (rows, EDGE), 1)
        for seg in range(local_segs):
            ring = jnp.where(lane < EDGE // 2, high[step, seg], low[step, seg])
            line = jnp.concatenate([maps[step, seg], ring], axis=1)
            width = bins + EDGE
            for shift in range(-HALO, HALO + 1):
                turned = line if shift == 0 else pltpu.roll(line, (-shift) % width, 1)
                shifted[seg, HALO + shift] = turned[:, :bins]

        def spindown(spin, carry):
            value = total[spin]
            for seg in range(local_segs):
                value = value + shifted[seg, HALO + offsets[spin, first + seg]]
            total[spin] = value
            return carry

        lax.fori_loop(0, spins, spindown, 0, unroll=2)

    own.wait()
    forward(0)

    @pl.loop(1, nseg)
    def _(step):
        exchange(step).wait_recv()
        forward(step)
        add(step - 1)

    add(nseg - 1)

    best = total[0]
    for spin in range(1, spins):
        best = jnp.maximum(best, total[spin])
    top = jnp.max(best, axis=1, keepdims=True) * (1.0 / (nseg * local_segs))
    tops[0] = jnp.broadcast_to(top, (rows, EDGE))

    def tell(step):
        return pltpu.make_async_remote_copy(
            src_ref=tops.at[0],
            dst_ref=tops.at[step],
            send_sem=top_send.at[step],
            recv_sem=top_recv.at[step],
            device_id={"seg": me, "freq": lax.rem(band + step, nfreq)},
            device_id_type=MESH,
        )

    for step in range(1, nfreq):
        tell(step).start()

    @pl.loop(1, nseg)
    def _(step):
        exchange(step).wait_send()

    @pl.loop(0, nseg)
    def _(step):
        @pl.when(band < nfreq - 1)
        def _():
            upward(step).wait_send()

        @pl.when(band > 0)
        def _():
            downward(step).wait_send()

    for step in range(1, nfreq):
        tell(step).wait()
    peak = tops[0]
    for step in range(1, nfreq):
        peak = jnp.maximum(peak, tops[step])
    peaks[...] = peak


def solution(mesh):
    nseg, nfreq = mesh.shape["seg"], mesh.shape["freq"]

    def on_device(coarse, offsets):
        local_segs, points, bins = coarse.shape
        rows = points // nseg
        spins = offsets.shape[1]
        total, peaks = pl.pallas_call(
            functools.partial(kernel, nseg, nfreq),
            out_shape=(
                jax.ShapeDtypeStruct((spins, rows, bins), jnp.float32),
                jax.ShapeDtypeStruct((rows, EDGE), jnp.float32),
            ),
            in_specs=[
                pl.BlockSpec(memory_space=pl.ANY),
                pl.BlockSpec(memory_space=pltpu.SMEM),
            ],
            out_specs=(
                pl.BlockSpec(memory_space=pltpu.VMEM),
                pl.BlockSpec(memory_space=pltpu.VMEM),
            ),
            scratch_shapes=[
                pltpu.VMEM((nseg, local_segs, rows, bins), jnp.float32),
                pltpu.VMEM((nseg, local_segs, rows, EDGE), jnp.float32),
                pltpu.VMEM((nseg, local_segs, rows, EDGE), jnp.float32),
                pltpu.VMEM((local_segs, SHIFTS, rows, bins), jnp.float32),
                pltpu.VMEM((nfreq, rows, EDGE), jnp.float32),
                pltpu.SemaphoreType.DMA,
                pltpu.SemaphoreType.DMA((nseg,)),
                pltpu.SemaphoreType.DMA((nseg,)),
                pltpu.SemaphoreType.DMA((nseg,)),
                pltpu.SemaphoreType.DMA((nseg,)),
                pltpu.SemaphoreType.DMA((nseg,)),
                pltpu.SemaphoreType.DMA((nseg,)),
                pltpu.SemaphoreType.DMA((nfreq,)),
                pltpu.SemaphoreType.DMA((nfreq,)),
            ],
            compiler_params=pltpu.CompilerParams(collective_id=0, has_side_effects=True),
        )(coarse, offsets.T)
        return total * (1.0 / (nseg * local_segs)), peaks[:, 0]

    return jax.shard_map(
        on_device,
        mesh=mesh,
        in_specs=(P("seg", None, "freq"), P()),
        out_specs=(P(None, "seg", "freq"), P("seg")),
        check_vma=False,
    )
```

time: 126 us -> 63.3 us (0.50); the launches traced: 124 us -> 62.8 us
  Pallas kernels: 0 us -> 59.2 us
  blocking collectives: 59.2 us -> 0 us
  matrix products: 35.6 us -> 0 us
  local copies, waits for them, and re-layouts: 19.5 us -> 0.63 us
  starting transfers between devices: 5.59 us -> 0 us
  waiting for transfers between devices: 3.14 us -> 0 us
  other arithmetic: 0 us -> 2.31 us
    pallas_call x0 -> x1, Pallas kernels: none -> 59.2 us  [on_device(): pl.pallas_call(functools.partial(kernel, nseg, nfreq), out_shape=(jax.Sha...]
    all_to_all x1 -> x0, blocking collectives: 53.3 us -> none  [on_device(): lax.all_to_all(blocks, 'seg', split_axis=1, concat_axis=0, tiled=True)[:, 0]]
    dot_general x17 -> x0, matrix products: 35.6 us -> none  [shift_sum(): jnp.einsum('ks,spw->kpw', weights, padded, precision=lax.Precision.HIGHES...]
    concatenate x2 -> x0, local copies, waits for them, and re-layouts: 10.3 us -> none  [extended(): block = jnp.concatenate([low, block, high], axis=dim)]
    pmax x1 -> x0, blocking collectives: 5.97 us -> none  [on_device(): peaks = lax.pmax(top_rows[0], 'freq')]
    ppermute x2 -> x0, starting transfers between devices: 5.59 us -> none  [the longest x1 4.13 us: extended(): lax.ppermute(lax.slice_in_dim(block, block.shape[dim] - width, None, axis...]
    unnamed x22 -> x2, local copies, waits for them, and re-layouts: 4.8 us -> 0.01 us
    ppermute x2 -> x0, waiting for transfers between devices: 3.14 us -> none  [the longest x1 3.14 us: extended(): lax.ppermute(lax.slice_in_dim(block, block.shape[dim] - width, None, axis...]
  transfers between devices with their start and end apart: 2 -> 0, of which waited for: 1 -> 0; matrix products, arithmetic and copies ran while one was open for 18% -> 0% of each run, Pallas kernels for 0% -> 0%
where the time goes in v1:
time: 63.3 us; the launch traced here: 62.8 us
  Pallas kernels  59.2 us (94%)
  other arithmetic  2.31 us (4%)
  between operations  0.65 us (1%)
    pallas_call x1, Pallas kernels, on_device(): pl.pallas_call(functools.partial(kernel, nseg, nfreq), out_shape=(jax.Sha...  59.2 us
    mul x1, other arithmetic, on_device(): return (total * (1.0 / (nseg * local_segs)), peaks[:, 0])  2.31 us

profile of v1, /device:TPU:8, one launch (start us, length us, event | category | flops | bytes accessed | tf_op | source)
XLA Modules:
  0.0 62.8 jit_solution(3909321265937608529)
XLA Ops:
  0.6 59.2 %shard_map.41 = (f32[32,8,1024]{2,1,0:T(8,128)}, f32[8,128]{1,0:T(8,128)}) custom-call(f32[4,128,1024]{2,1,0:T(8,128)} %coarse.1, s32[32,64]{1,0:T(8,128)} %bitcast.1), custom_call_target="tpu_custom_call" | custom-call | tf_op jit(solution)/shard_map/pallas_call | solution.py:218
  59.9 0.0 copy-start
  59.9 2.3 %broadcast_multiply_fusion = f32[32,8,1024]{2,1,0:T(8,128)} fusion(f32[32,8,1024]{2,1,0:T(8,128)} %get-tuple-element.4), kind=kLoop, calls=%fused_computation | loop fusion | flops 262144 | bytes 2097152 | tf_op jit(solution)/shard_map/mul | solution.py:250
  62.2 0.0 copy-done
  62.2 0.6 slice_reduce_fusion
Async XLA Ops:
  59.9 2.3 %copy-start = (f32[8,128]{1,0:T(8,128)S(1)}, f32[8,128]{1,0:T(8,128)}, u32[]{:S(2)}) copy-start(f32[8,128]{1,0:T(8,128)} %get-tuple-element.5) | copy-start | bytes 12292

commit v2 on v1

--- a/solution.py
+++ b/solution.py
@@ -38,7 +38,11 @@
     high,
     shifted,
     tops,
+    shifts,
     own_sem,
+    shifts_sem,
+    edge_sem,
+    edge_recv,
     send_sem,
     recv_sem,
     up_send,
@@ -56,16 +60,28 @@
     def mine(target):
         return coarse.at[:, pl.ds(pl.multiple_of(target * rows, rows), rows), :]
 
-    def exchange(step):
+    early = EDGE if nfreq == 2 else bins
+    edge_at = jnp.where(band == 0, bins - early, 0)
+    rest_at = jnp.where(band == 0, 0, early)
+
+    def piece(step, begin, size, sent, received):
         other = partner(me, step, nseg)
-        return pltpu.make_async_remote_copy(
-            src_ref=mine(other),
-            dst_ref=maps.at[step],
-            send_sem=send_sem.at[step],
-            recv_sem=recv_sem.at[step],
+        columns = pl.ds(pl.multiple_of(begin, EDGE), size)
+        rows_of = pl.ds(pl.multiple_of(other * rows, rows), rows)
+        return pltpu.make_async_remote_copy(
+            src_ref=coarse.at[:, rows_of, columns],
+            dst_ref=maps.at[step, :, :, columns],
+            send_sem=sent.at[step],
+            recv_sem=received.at[step],
             device_id={"seg": other, "freq": band},
             device_id_type=MESH,
         )
+
+    def edge(step):
+        return piece(step, edge_at, early, edge_sem, edge_recv)
+
+    def rest(step):
+        return piece(step, rest_at, bins - early, send_sem, recv_sem)
 
     def upward(step):
         return pltpu.make_async_remote_copy(
@@ -103,6 +119,8 @@
             barrier, inc=1, device_id={"seg": me, "freq": lax.rem(band + step, nfreq)}, device_id_type=MESH
         )
 
+    load_shifts = pltpu.make_async_copy(offsets, shifts, shifts_sem)
+    load_shifts.start()
     total[...] = jnp.zeros_like(total)
 
     @pl.when(band == 0)
@@ -117,7 +135,13 @@
 
     @pl.loop(1, nseg)
     def _(step):
-        exchange(step).start()
+        edge(step).start()
+
+    if early < bins:
+
+        @pl.loop(1, nseg)
+        def _(step):
+            rest(step).start()
 
     def forward(step):
         @pl.when(band < nfreq - 1)
@@ -150,7 +174,7 @@
         def spindown(spin, carry):
             value = total[spin]
             for seg in range(local_segs):
-                value = value + shifted[seg, HALO + offsets[spin, first + seg]]
+                value = value + shifted[seg, HALO + shifts[spin, first + seg]]
             total[spin] = value
             return carry
 
@@ -161,11 +185,17 @@
 
     @pl.loop(1, nseg)
     def _(step):
-        exchange(step).wait_recv()
+        edge(step).wait_recv()
         forward(step)
-        add(step - 1)
-
-    add(nseg - 1)
+
+    load_shifts.wait()
+    add(0)
+
+    @pl.loop(1, nseg)
+    def _(step):
+        if early < bins:
+            rest(step).wait_recv()
+        add(step)
 
     best = total[0]
     for spin in range(1, spins):
@@ -188,7 +218,9 @@
 
     @pl.loop(1, nseg)
     def _(step):
-        exchange(step).wait_send()
+        edge(step).wait_send()
+        if early < bins:
+            rest(step).wait_send()
 
     @pl.loop(0, nseg)
     def _(step):
@@ -222,8 +254,8 @@
                 jax.ShapeDtypeStruct((rows, EDGE), jnp.float32),
             ),
             in_specs=[
-                pl.BlockSpec(memory_space=pl.ANY),
-                pl.BlockSpec(memory_space=pltpu.SMEM),
+                pl.BlockSpec(memory_space=pltpu.HBM),
+                pl.BlockSpec(memory_space=pltpu.HBM),
             ],
             out_specs=(
                 pl.BlockSpec(memory_space=pltpu.VMEM),
@@ -235,7 +267,11 @@
                 pltpu.VMEM((nseg, local_segs, rows, EDGE), jnp.float32),
                 pltpu.VMEM((local_segs, SHIFTS, rows, bins), jnp.float32),
                 pltpu.VMEM((nfreq, rows, EDGE), jnp.float32),
+                pltpu.SMEM(offsets.shape[::-1], jnp.int32),
                 pltpu.SemaphoreType.DMA,
+                pltpu.SemaphoreType.DMA,
+                pltpu.SemaphoreType.DMA((nseg,)),
+                pltpu.SemaphoreType.DMA((nseg,)),
                 pltpu.SemaphoreType.DMA((nseg,)),
                 pltpu.SemaphoreType.DMA((nseg,)),
                 pltpu.SemaphoreType.DMA((nseg,)),
@@ -245,8 +281,10 @@
                 pltpu.SemaphoreType.DMA((nfreq,)),
                 pltpu.SemaphoreType.DMA((nfreq,)),
             ],
-            compiler_params=pltpu.CompilerParams(collective_id=0, has_side_effects=True),
-        )(coarse, offsets.T)
+            compiler_params=pltpu.CompilerParams(
+                collective_id=0, has_side_effects=True, vmem_limit_bytes=32 << 20
+            ),
+        )(pltpu.with_memory_space_constraint(coarse, pltpu.HBM), pltpu.with_memory_space_constraint(offsets.T, pltpu.HBM))
         return total * (1.0 / (nseg * local_segs)), peaks[:, 0]
 
     return jax.shard_map(

time: 63.3 us -> 58.1 us (0.918)
  Pallas kernels: 59.2 us -> 55.5 us
  other arithmetic: 2.31 us -> 1.09 us
    pallas_call x1, Pallas kernels: 59.2 us -> 55.5 us  [on_device(): pl.pallas_call(functools.partial(kernel, nseg, nfreq), out_shape=(jax.Sha...]
    mul x1, other arithmetic: 2.31 us -> 1.09 us  [on_device(): return (total * (1.0 / (nseg * local_segs)), peaks[:, 0])]
where the time goes in v2:
time: 58.1 us; the launch traced here: 57.8 us
  Pallas kernels  55.5 us (96%)
  other arithmetic  1.09 us (2%)
  between operations  0.64 us (1%)
  local copies, waits for them, and re-layouts  0.62 us (1%)
    pallas_call x1, Pallas kernels, on_device(): pl.pallas_call(functools.partial(kernel, nseg, nfreq), out_shape=(jax.Sha...  55.5 us

profile of v2, /device:TPU:8, one launch (start us, length us, event | category | flops | bytes accessed | tf_op | source)
XLA Modules:
  0.0 57.8 jit_solution(6013029435378315717)
XLA Ops:
  0.6 55.5 %shard_map.41 = (f32[32,8,1024]{2,1,0:T(8,128)S(1)}, f32[8,128]{1,0:T(8,128)S(1)}) custom-call(f32[4,128,1024]{2,1,0:T(8,128)} %coarse.1, s32[32,64]{1,0:T(8,128)} %bitcast.1), custom_call_target="tpu_custom_call" | custom-call | tf_op jit(solution)/shard_map/pallas_call | solution.py:250
  56.1 1.1 %broadcast_multiply_fusion = f32[32,8,1024]{2,1,0:T(8,128)} fusion(f32[32,8,1024]{2,1,0:T(8,128)S(1)} %get-tuple-element.4), kind=kLoop, calls=%fused_computation | loop fusion | flops 262144 | bytes 2097152 | tf_op jit(solution)/shard_map/mul | solution.py:288
  57.2 0.6 %slice_reduce_fusion = f32[8]{0:T(128)} fusion(f32[8,128]{1,0:T(8,128)S(1)} %get-tuple-element.5), kind=kLoop, calls=%fused_computation.1 | loop fusion | bytes 64 | tf_op jit(solution)/shard_map/slice | solution.py:288

commit v3 on v2

--- a/solution.py
+++ b/solution.py
@@ -19,7 +19,7 @@
     result = me
     bit = 1
     while bit < count:
-        wanted = lax.rem(step // bit, 2)
+        wanted = (step // bit) % 2 if isinstance(step, int) else lax.rem(step // bit, 2)
         held = lax.rem(me // bit, 2)
         result = result + bit * wanted * (1 - 2 * held)
         bit *= 2
@@ -54,6 +54,9 @@
 ):
     local_segs = coarse.shape[0]
     spins, rows, bins = total.shape
+    parts = recv_sem.shape[0]
+    part_segs = local_segs // parts
+    scale = 1.0 / (nseg * local_segs)
     me = lax.axis_index("seg")
     band = lax.axis_index("freq")
 
@@ -64,24 +67,25 @@
     edge_at = jnp.where(band == 0, bins - early, 0)
     rest_at = jnp.where(band == 0, 0, early)
 
-    def piece(step, begin, size, sent, received):
+    def piece(step, begin, size, segs, sent, received):
         other = partner(me, step, nseg)
         columns = pl.ds(pl.multiple_of(begin, EDGE), size)
         rows_of = pl.ds(pl.multiple_of(other * rows, rows), rows)
         return pltpu.make_async_remote_copy(
-            src_ref=coarse.at[:, rows_of, columns],
-            dst_ref=maps.at[step, :, :, columns],
-            send_sem=sent.at[step],
-            recv_sem=received.at[step],
+            src_ref=coarse.at[segs, rows_of, columns],
+            dst_ref=maps.at[step, segs, :, columns],
+            send_sem=sent,
+            recv_sem=received,
             device_id={"seg": other, "freq": band},
             device_id_type=MESH,
         )
 
     def edge(step):
-        return piece(step, edge_at, early, edge_sem, edge_recv)
-
-    def rest(step):
-        return piece(step, rest_at, bins - early, send_sem, recv_sem)
+        return piece(step, edge_at, early, pl.ds(0, local_segs), edge_sem.at[step], edge_recv.at[step])
+
+    def rest(step, part):
+        segs = pl.ds(part * part_segs, part_segs)
+        return piece(step, rest_at, bins - early, segs, send_sem.at[part, step], recv_sem.at[part, step])
 
     def upward(step):
         return pltpu.make_async_remote_copy(
@@ -108,8 +112,7 @@
 
     barrier = pltpu.get_barrier_semaphore()
 
-    @pl.loop(1, nseg)
-    def _(step):
+    for step in reversed(range(1, nseg)):
         pl.semaphore_signal(
             barrier, inc=1, device_id={"seg": partner(me, step, nseg), "freq": band}, device_id_type=MESH
         )
@@ -141,7 +144,8 @@
 
         @pl.loop(1, nseg)
         def _(step):
-            rest(step).start()
+            for part in range(parts):
+                rest(step, part).start()
 
     def forward(step):
         @pl.when(band < nfreq - 1)
@@ -152,7 +156,7 @@
         def _():
             downward(step).start()
 
-    def add(step):
+    def wait_edges(step):
         @pl.when(band < nfreq - 1)
         def _():
             downward(step).wait_recv()
@@ -161,9 +165,11 @@
         def _():
             upward(step).wait_recv()
 
+    def add(step, part, best=None):
         first = partner(me, step, nseg) * local_segs
+        segs = range(part * part_segs, (part + 1) * part_segs)
         lane = lax.broadcasted_iota(jnp.int32, (rows, EDGE), 1)
-        for seg in range(local_segs):
+        for seg in segs:
             ring = jnp.where(lane < EDGE // 2, high[step, seg], low[step, seg])
             line = jnp.concatenate([maps[step, seg], ring], axis=1)
             width = bins + EDGE
@@ -171,14 +177,17 @@
                 turned = line if shift == 0 else pltpu.roll(line, (-shift) % width, 1)
                 shifted[seg, HALO + shift] = turned[:, :bins]
 
-        def spindown(spin, carry):
+        def spindown(spin, best):
             value = total[spin]
-            for seg in range(local_segs):
+            for seg in segs:
                 value = value + shifted[seg, HALO + shifts[spin, first + seg]]
+            if best is not None:
+                value = value * scale
+                best = jnp.maximum(best, value)
             total[spin] = value
-            return carry
-
-        lax.fori_loop(0, spins, spindown, 0, unroll=2)
+            return best
+
+        return lax.fori_loop(0, spins, spindown, best, unroll=4)
 
     own.wait()
     forward(0)
@@ -189,19 +198,28 @@
         forward(step)
 
     load_shifts.wait()
-    add(0)
-
-    @pl.loop(1, nseg)
-    def _(step):
-        if early < bins:
-            rest(step).wait_recv()
-        add(step)
-
-    best = total[0]
-    for spin in range(1, spins):
-        best = jnp.maximum(best, total[spin])
-    top = jnp.max(best, axis=1, keepdims=True) * (1.0 / (nseg * local_segs))
-    tops[0] = jnp.broadcast_to(top, (rows, EDGE))
+    wait_edges(0)
+    for part in range(parts):
+        add(0, part)
+
+    def receive(step, best=None):
+        wait_edges(step)
+        for part in range(parts):
+            if early < bins:
+                rest(step, part).wait_recv()
+            last = best if part == parts - 1 else None
+            result = add(step, part, last)
+        return result
+
+    @pl.loop(1, nseg - 1)
+    def _(step):
+        receive(step)
+
+    best = receive(nseg - 1, jnp.full((rows, bins), -jnp.inf, jnp.float32))
+    top = best[:, :EDGE]
+    for begin in range(EDGE, bins, EDGE):
+        top = jnp.maximum(top, best[:, begin : begin + EDGE])
+    tops[0] = top
 
     def tell(step):
         return pltpu.make_async_remote_copy(
@@ -220,7 +238,8 @@
     def _(step):
         edge(step).wait_send()
         if early < bins:
-            rest(step).wait_send()
+            for part in range(parts):
+                rest(step, part).wait_send()
 
     @pl.loop(0, nseg)
     def _(step):
@@ -240,6 +259,18 @@
     peaks[...] = peak
 
 
+def finish(total, tops, fine, peaks, sem):
+    write = pltpu.make_async_copy(total, fine, sem)
+    write.start()
+    rows, width = tops.shape
+    row = lax.broadcasted_iota(jnp.int32, (rows, width), 0)
+    lane = lax.broadcasted_iota(jnp.int32, (rows, width), 1)
+    top = jnp.max(tops[...], axis=1, keepdims=True)
+    line = jnp.sum(jnp.where(row == lane, top, 0.0), axis=0)
+    peaks[...] = line[:rows]
+    write.wait()
+
+
 def solution(mesh):
     nseg, nfreq = mesh.shape["seg"], mesh.shape["freq"]
 
@@ -247,6 +278,7 @@
         local_segs, points, bins = coarse.shape
         rows = points // nseg
         spins = offsets.shape[1]
+        parts = 1
         total, peaks = pl.pallas_call(
             functools.partial(kernel, nseg, nfreq),
             out_shape=(
@@ -272,8 +304,8 @@
                 pltpu.SemaphoreType.DMA,
                 pltpu.SemaphoreType.DMA((nseg,)),
                 pltpu.SemaphoreType.DMA((nseg,)),
-                pltpu.SemaphoreType.DMA((nseg,)),
-                pltpu.SemaphoreType.DMA((nseg,)),
+                pltpu.SemaphoreType.DMA((parts, nseg)),
+                pltpu.SemaphoreType.DMA((parts, nseg)),
                 pltpu.SemaphoreType.DMA((nseg,)),
                 pltpu.SemaphoreType.DMA((nseg,)),
                 pltpu.SemaphoreType.DMA((nseg,)),
@@ -285,7 +317,17 @@
                 collective_id=0, has_side_effects=True, vmem_limit_bytes=32 << 20
             ),
         )(pltpu.with_memory_space_constraint(coarse, pltpu.HBM), pltpu.with_memory_space_constraint(offsets.T, pltpu.HBM))
-        return total * (1.0 / (nseg * local_segs)), peaks[:, 0]
+        return pl.pallas_call(
+            finish,
+            out_shape=(
+                jax.ShapeDtypeStruct((spins, rows, bins), jnp.float32),
+                jax.ShapeDtypeStruct((rows,), jnp.float32),
+            ),
+            in_specs=[pl.BlockSpec(memory_space=pltpu.VMEM), pl.BlockSpec(memory_space=pltpu.VMEM)],
+            out_specs=(pl.BlockSpec(memory_space=pltpu.HBM), pl.BlockSpec(memory_space=pltpu.VMEM)),
+            scratch_shapes=[pltpu.SemaphoreType.DMA],
+            compiler_params=pltpu.CompilerParams(vmem_limit_bytes=8 << 20),
+        )(total, peaks)
 
     return jax.shard_map(
         on_device,

time: 58.1 us -> 57.3 us (0.986)
  Pallas kernels: 55.5 us -> 56.6 us
  other arithmetic: 1.09 us -> 0 us
  local copies, waits for them, and re-layouts: 0.62 us -> 0 us
    pallas_call x0 -> x1, Pallas kernels: none -> 1.49 us  [on_device(): pl.pallas_call(finish, out_shape=(jax.ShapeDtypeStruct((spins, rows, bins...]
    mul x1 -> x0, other arithmetic: 1.09 us -> none  [on_device(): return (total * (1.0 / (nseg * local_segs)), peaks[:, 0])]
    slice x1 -> x0, local copies, waits for them, and re-layouts: 0.62 us -> none  [on_device(): return (total * (1.0 / (nseg * local_segs)), peaks[:, 0])]
where the time goes in v3:
time: 57.3 us; the launch traced here: 57.2 us
  Pallas kernels  56.6 us (99%)
  between operations  0.64 us (1%)
    pallas_call x1, Pallas kernels, on_device(): pl.pallas_call(functools.partial(kernel, nseg, nfreq), out_shape=(jax.Sha...  55.1 us
    pallas_call x1, Pallas kernels, on_device(): pl.pallas_call(finish, out_shape=(jax.ShapeDtypeStruct((spins, rows, bins...  1.49 us

profile of v3, /device:TPU:8, one launch (start us, length us, event | category | flops | bytes accessed | tf_op | source)
XLA Modules:
  0.0 57.2 jit_solution(15190645550577688792)
XLA Ops:
  0.6 55.1 %shard_map.41 = (f32[32,8,1024]{2,1,0:T(8,128)S(1)}, f32[8,128]{1,0:T(8,128)S(1)}) custom-call(f32[4,128,1024]{2,1,0:T(8,128)} %coarse.1, s32[32,64]{1,0:T(8,128)} %bitcast.1), custom_call_target="tpu_custom_call" | custom-call | tf_op jit(solution)/shard_map/pallas_call | solution.py:282
  55.7 1.5 %shard_map.42 = (f32[32,8,1024]{2,1,0:T(8,128)}, f32[8]{0:T(128)}) custom-call(f32[32,8,1024]{2,1,0:T(8,128)S(1)} %get-tuple-element.4.total, f32[8,128]{1,0:T(8,128)S(1)} %get-tuple-element.5.tops), custom_call_target="tpu_custom_call" | custom-call | tf_op jit(solution)/shard_map/pallas_call | solution.py:320
